TPU v7x, 32 devices: a whole 2x2x4 slice. The times are simulated.
32 devices in a mesh: ep: 4 (over y, x), fsdp: 8 (over z, core).
Axes of the slice: x: 2, y: 2, z: 4, core: 2. Of those that a mesh axis runs over, the one named last changes fastest.
Arguments:
- train_gate: float32 [64, 2048, 1408], P('ep', 'fsdp'), may hold values from -0.1875 to 0.1875
- other_gate: bfloat16 [64, 2048, 1408], P('ep', 'fsdp'), may hold values from -0.0625 to 0.0625
- train_up: float32 [64, 2048, 1408], P('ep', 'fsdp'), may hold values from -0.1875 to 0.1875
- other_up: bfloat16 [64, 2048, 1408], P('ep', 'fsdp'), may hold values from -0.0625 to 0.0625
- router_weight: float32 [2048, 64], P('fsdp', 'ep'), may hold values from -0.125 to 0.125
- router_gain: float32 [2048], P('fsdp'), may hold values from 0.25 to 1.75
Outputs:
- ready_gate: bfloat16 [64, 2048, 1408], P('ep', None, 'fsdp')
- ready_up: bfloat16 [64, 2048, 1408], P('ep', None, 'fsdp')
- scale_gate: float32 [64, 1408], P('ep', 'fsdp')
- scale_up: float32 [64, 1408], P('ep', 'fsdp')
- serve_router: bfloat16 [2048, 64], replicated
All inputs are finite; a program needn't handle non-finite values. Where the computation divides by a largest or mean magnitude, that divisor is 1e-20 or more.
Results may differ from a plain program's by a relative error of at most 0.001.
Values may be sent and summed in bfloat16 or wider, within the bound.
A program may use at most 192 MiB of HBM per device.

v0:
```python
import jax
import jax.numpy as jnp
from jax import lax
from jax.sharding import PartitionSpec as P


def per_device(train_gate, other_gate, train_up, other_up, router_weight, router_gain):
    latest_gate = train_gate + other_gate.astype(jnp.float32)
    latest_up = train_up + other_up.astype(jnp.float32)
    scale_gate, scale_up = lax.pmax(
        (jnp.max(jnp.abs(latest_gate), axis=1), jnp.max(jnp.abs(latest_up), axis=1)), "fsdp"
    )
    narrow_gate, narrow_up = (
        (latest_gate / jnp.expand_dims(scale_gate, 1)).astype(jnp.bfloat16),
        (latest_up / jnp.expand_dims(scale_up, 1)).astype(jnp.bfloat16),
    )
    ready_gate, ready_up = (
        lax.all_to_all(narrow_gate, "fsdp", split_axis=2, concat_axis=1, tiled=True),
        lax.all_to_all(narrow_up, "fsdp", split_axis=2, concat_axis=1, tiled=True),
    )
    scale_gate = lax.dynamic_slice_in_dim(
        scale_gate, lax.axis_index("fsdp") * ready_gate.shape[2], ready_gate.shape[2], axis=1
    )
    scale_up = lax.dynamic_slice_in_dim(
        scale_up, lax.axis_index("fsdp") * ready_up.shape[2], ready_up.shape[2], axis=1
    )
    part_router = (router_weight * router_gain[:, None]).astype(jnp.bfloat16)
    row_router = lax.all_gather(part_router, "fsdp", axis=0, tiled=True)
    serve_router = lax.all_gather(row_router, "ep", axis=1, tiled=True)
    return (ready_gate, ready_up, scale_gate, scale_up, serve_router)


def solution(mesh):
    in_specs = (
        P("ep", "fsdp", None),
        P("ep", "fsdp", None),
        P("ep", "fsdp", None),
        P("ep", "fsdp", None),
        P("fsdp", "ep"),
        P("fsdp"),
    )
    out_specs = (
        P("ep", None, "fsdp"),
        P("ep", None, "fsdp"),
        P("ep", "fsdp"),
        P("ep", "fsdp"),
        P(),
    )
    return jax.shard_map(
        per_device, mesh=mesh, in_specs=in_specs, out_specs=out_specs, check_vma=False
    )
```

profile of v0, /device:TPU:0, one launch (start us, length us, event | category | flops | bytes accessed | tf_op | source)
XLA Modules:
  0.0 809.5 jit_solution(1631548331659294860)
XLA Ops:
  7.2 0.0 all-reduce.3.cloned.1.call-start
  7.2 23.7 %copy.38 = f32[16,256,1408]{1,0,2:T(8,128)} copy(f32[16,256,1408]{2,1,0:T(8,128)} %param.8) | data formatting | bytes 46137344 | tf_op args[2]
  30.9 16.4 %copy.37 = bf16[16,256,1408]{1,0,2:T(8,128)(2,1)} copy(bf16[16,256,1408]{2,1,0:T(8,128)(2,1)} %param.9) | data formatting | bytes 23068672 | tf_op args[3]
  47.2 23.7 %copy.34 = f32[16,256,1408]{1,0,2:T(8,128)} copy(f32[16,256,1408]{2,1,0:T(8,128)} %param.6) | data formatting | bytes 46137344 | tf_op args[0]
  70.9 16.4 %copy.33 = bf16[16,256,1408]{1,0,2:T(8,128)(2,1)} copy(bf16[16,256,1408]{2,1,0:T(8,128)(2,1)} %param.7) | data formatting | bytes 23068672 | tf_op args[1]
  87.3 0.0 copy-start
  87.3 0.0 copy-start.1
  87.3 20.8 %abs_reduce_fusion = f32[16,1408]{0,1:T(8,128)} fusion(f32[16,256,1408]{1,0,2:T(8,128)} %copy.38, bf16[16,256,1408]{1,0,2:T(8,128)(2,1)} %copy.37), kind=kLoop, calls=%fused_computation.1 | loop fusion | flops 23046144 | bytes 34693120 | tf_op jit(solution)/shard_map/reduce_max | solution.py:11
  108.1 0.0 copy-done
  108.1 0.0 copy-done.1
  108.1 14.9 %abs_reduce_fusion.1 = f32[16,1408]{0,1:T(8,128)} fusion(f32[16,256,1408]{1,0,2:T(8,128)S(1)} %copy-done, bf16[16,256,1408]{1,0,2:T(8,128)(2,1)S(1)} %copy-done.1), kind=kLoop, calls=%fused_computation.4 | loop fusion | flops 23046144 | bytes 34693120 | tf_op jit(solution)/shard_map/reduce_max | solution.py:11
  123.0 0.0 all-reduce.3.cloned.1.call-update
  123.0 64.1 %all-reduce.3.cloned.1.call-done = (f32[16,1408]{0,1:T(8,128)}, f32[16,1408]{0,1:T(8,128)}) async-done(((f32[16,1408]{0,1:T(8,128)}, f32[16,1408]{0,1:T(8,128)}), (f32[16,1408]{0,1:T(8,128)}, f32[16,1408]{0,1:T(8,128)})) %all-reduce.3.cloned.1.call-update) | async-done | bytes 180240 | tf_op jit(solution)/shard_map/pmax | solution.py:10
  187.2 27.3 %divide_convert_fusion = (bf16[16,256,1408]{1,0,2:T(8,128)(2,1)}, bf16[16,256,1408]{1,0,2:T(8,128)(2,1)S(1)}) fusion(f32[16,256,1408]{1,0,2:T(8,128)} %copy.38, bf16[16,256,1408]{1,0,2:T(8,128)(2,1)} %copy.37, f32[16,1408]{0,1:T(8,128)} %get-tuple-element.11, f32[16,1408]{0,1:T(8,128)} %get-tuple-element.10, f32[16,256,1408]{1,0,2:T(8,128)} %copy.34, ...), kind=kLoop, calls=%fused_computation | loop fusion | flops 46137344 | bytes 92454912 | tf_op jit(solution)/shard_map/convert_element_type | solution.py:15
  214.5 0.0 copy-start.2
  214.5 0.0 copy-start.3
  214.5 255.0 %all_to_all.36 = bf16[16,256,1408]{1,0,2:T(8,128)(2,1)} all-to-all(bf16[16,256,1408]{1,0,2:T(8,128)(2,1)S(1)} %get-tuple-element.13), channel_id=1, replica_groups=mesh['ep'=4,'fsdp'=8] {'fsdp'}, dimensions={2} | all-to-all | bytes 23068672 | tf_op jit(solution)/shard_map/all_to_all | solution.py:18
  469.5 5.3 all-to-all-start.1
  474.8 0.0 copy-done.2
  474.8 0.0 copy-done.3
  474.8 257.3 %all_gather.6 = bf16[2048,16]{0,1:T(8,128)(2,1)S(1)} all-gather(bf16[256,16]{0,1:T(8,128)(2,1)S(1)} %multiply_convert_fusion), channel_id=1, replica_groups=mesh['ep'=4,'fsdp'=8] {'fsdp'}, dimensions={0}, use_global_device_ids=true | all-gather | bytes 73728 | tf_op jit(solution)/shard_map/all_gather | solution.py:28
  732.1 8.9 %all_gather.7 = bf16[2048,64]{0,1:T(8,128)(2,1)S(1)} all-gather(bf16[2048,16]{0,1:T(8,128)(2,1)S(1)} %all_gather.6), channel_id=1, replica_groups=mesh['ep'=4,'fsdp'=8] {'ep'}, dimensions={1}, use_global_device_ids=true | all-gather | bytes 327680 | tf_op jit(solution)/shard_map/all_gather | solution.py:29
  741.0 0.9 constant_dynamic-slice_fusion
  742.0 0.7 copy.41
  742.6 0.7 copy.42
  743.3 11.3 %copy.36 = bf16[16,8,256,176]{2,1,3,0:T(8,128)(2,1)} copy(bf16[16,8,256,176]{2,0,3,1:T(8,128)(2,1)} %bitcast.14) | data formatting | bytes 23068672 | tf_op jit(solution)/shard_map/all_to_all | solution.py:18
  754.7 18.0 %all_to_all.29 = bf16[16,2048,176]{1,2,0:T(8,128)(2,1)} reshape(bf16[16,8,256,176]{2,1,3,0:T(8,128)(2,1)} %copy.36) | data formatting | bytes 23068672 | tf_op jit(solution)/shard_map/all_to_all | solution.py:18
  772.6 0.0 all-to-all-done.1
  772.6 11.4 %copy.40 = bf16[16,8,256,176]{2,1,3,0:T(8,128)(2,1)} copy(bf16[16,8,256,176]{2,0,3,1:T(8,128)(2,1)} %bitcast.5) | data formatting | bytes 23068672 | tf_op jit(solution)/shard_map/all_to_all | solution.py:19
  784.0 18.0 %all_to_all.33 = bf16[16,2048,176]{1,2,0:T(8,128)(2,1)} reshape(bf16[16,8,256,176]{2,1,3,0:T(8,128)(2,1)} %copy.40) | data formatting | bytes 23068672 | tf_op jit(solution)/shard_map/all_to_all | solution.py:19
  802.0 0.7 copy.48
  (1 shorter events, 0.0 us)
Async XLA Ops:
  7.2 180.0 %all-reduce.3.cloned.1.call-start = ((), (), s32[]{:S(2)}) async-start(), calls=%async_computation.2 | async-start | bytes 2883584 | tf_op jit(solution)/shard_map/pmax | solution.py:10
  87.3 20.8 %copy-start = (f32[16,256,1408]{1,0,2:T(8,128)S(1)}, f32[16,256,1408]{1,0,2:T(8,128)}, u32[]{:S(2)}) copy-start(f32[16,256,1408]{1,0,2:T(8,128)} %copy.34) | copy-start | bytes 69206016
  87.3 20.9 %copy-start.1 = (bf16[16,256,1408]{1,0,2:T(8,128)(2,1)S(1)}, bf16[16,256,1408]{1,0,2:T(8,128)(2,1)}, u32[]{:S(2)}) copy-start(bf16[16,256,1408]{1,0,2:T(8,128)(2,1)} %copy.33) | copy-start | bytes 34603012
  214.5 260.3 %copy-start.2 = (f32[256,16]{0,1:T(8,128)S(1)}, f32[256,16]{0,1:T(8,128)}, u32[]{:S(2)}) copy-start(f32[256,16]{0,1:T(8,128)} %param.10) | copy-start | bytes 49156
  214.5 260.3 %copy-start.3 = (f32[256]{0:T(256)S(1)}, f32[256]{0:T(256)}, u32[]{:S(2)}) copy-start(f32[256]{0:T(256)} %param.11) | copy-start | bytes 3076
  469.5 303.1 %all-to-all-start.1 = ((bf16[16,256,1408]{1,0,2:T(8,128)(2,1)}), bf16[16,256,1408]{1,0,2:T(8,128)(2,1)}, u32[]{:S(2)}, u32[]{:S(2)}) async-start(bf16[16,256,1408]{1,0,2:T(8,128)(2,1)} %get-tuple-element.12), calls=%async_computation.1 | async-start | bytes 23068672 | tf_op jit(solution)/shard_map/all_to_all | solution.py:19
Sparse Core Ops, SparseCore 0:
  123.2 63.9 all-reduce.2
where the time goes:
time: 812 us; the launch traced here: 810 us
  blocking collectives  521 us (64%)
  local copies, waits for them, and re-layouts  142 us (17%)
  waiting for transfers between devices  64.2 us (8%)
  other arithmetic  63 us (8%)
  between operations  14.1 us (2%)
    all_gather x1, blocking collectives, per_device(): row_router = lax.all_gather(part_router, 'fsdp', axis=0, tiled=True)  257 us
    all_to_all x1, blocking collectives, per_device(): lax.all_to_all(narrow_gate, 'fsdp', split_axis=2, concat_axis=1, tiled=True)  255 us
    unnamed x15, local copies, waits for them, and re-layouts  82.2 us
    pmax x1, waiting for transfers between devices, per_device(): lax.pmax((jnp.max(jnp.abs(latest_gate), axis=1), jnp.max(jnp.abs(latest_u...  64.1 us
    all_to_all x2, local copies, waits for them, and re-layouts, per_device(): lax.all_to_all(narrow_up, 'fsdp', split_axis=2, concat_axis=1, tiled=True)  29.3 us
    all_to_all x2, local copies, waits for them, and re-layouts, per_device(): lax.all_to_all(narrow_gate, 'fsdp', split_axis=2, concat_axis=1, tiled=True)  29.3 us
    convert_element_type x1, other arithmetic, per_device(): (latest_up / jnp.expand_dims(scale_up, 1)).astype(jnp.bfloat16)  27.3 us
    reduce_max x1, other arithmetic, per_device(): jnp.max(jnp.abs(latest_up), axis=1)  20.8 us
  transfers between devices with their start and end apart: 2, of which 1 were waited for; matrix products, arithmetic and copies ran while one was open for 2% of the time, Pallas kernels for 0%

commit v1 on v0

v1 whole, which is shorter than its diff:
```python
import functools

import jax
import jax.numpy as jnp
from jax import lax
from jax.experimental import pallas as pl
from jax.experimental.pallas import tpu as pltpu
from jax.sharding import PartitionSpec as P

LANES = 128
DEPTH = 3


def regroup(n, tg, og, tu, ou, rg, ru, scales, mx, mo, nx, no, turned, blocks, own, pair, both, chips, final,
            mx_sem, mo_sem, nx_sem, no_sem, send_sem, keep_sem, recv_sem, p_send, p_recv, z_send, z_recv, f_send, f_recv, s_sem):
    me = lax.axis_index("fsdp")
    core = lax.rem(me, 2)
    partner = me + 1 - 2 * core
    experts, rows, columns = tg.shape
    width = columns // n
    trains, others, outs = (tg, tu), (og, ou), (rg, ru)

    def loads(x, o, x_sem, o_sem, e):
        slot = lax.rem(e, 2)
        copies = []
        for t in range(2):
            copies.append(pltpu.make_async_copy(trains[t].at[e], x.at[slot, t], x_sem.at[slot, t]))
            copies.append(pltpu.make_async_copy(others[t].at[e], o.at[slot, t], o_sem.at[slot, t]))
        return copies

    def remote(src, dst, send, recv, device):
        return pltpu.make_async_remote_copy(
            src_ref=src, dst_ref=dst, send_sem=send, recv_sem=recv, device_id={"fsdp": device},
            device_id_type=pl.DeviceIdType.MESH,
        )

    def wait_bytes(ref, sem):
        pltpu.make_async_copy(ref, ref, sem).wait()

    for copy in loads(mx, mo, mx_sem, mo_sem, 0):
        copy.start()
    for copy in loads(nx, no, nx_sem, no_sem, 0):
        copy.start()

    barrier = pltpu.get_barrier_semaphore()
    for k in range(1, n):
        pl.semaphore_signal(barrier, inc=1, device_id={"fsdp": lax.rem(me + k, n)}, device_id_type=pl.DeviceIdType.MESH)
    pl.semaphore_wait(barrier, n - 1)

    def measure(e):
        slot = lax.rem(e, 2)

        @pl.when(e + 1 < experts)
        def _():
            for copy in loads(mx, mo, mx_sem, mo_sem, e + 1):
                copy.start()

        for copy in loads(mx, mo, mx_sem, mo_sem, e):
            copy.wait()
        for t in range(2):
            for j in range(0, columns, LANES):
                latest = mx[slot, t, :, j : j + LANES] + mo[slot, t, :, j : j + LANES].astype(jnp.float32)
                own[e, t, :, j : j + LANES] = jnp.max(jnp.abs(latest), axis=0, keepdims=True)
        remote(own.at[e, 1 - core], pair.at[e], p_send.at[e], p_recv.at[e], partner).start()

    def chip_max(e):
        remote(own.at[e, 1 - core], pair.at[e], p_send.at[e], p_recv.at[e], partner).wait()
        both[e] = jnp.maximum(own[e, core], pair[e])
        for k in range(1, n // 2):
            remote(both.at[e], chips.at[e, k - 1], z_send.at[e], z_recv.at[e], lax.rem(me + 2 * k, n)).start()

    def all_max(e):
        wait_bytes(chips.at[e], z_send.at[e])
        wait_bytes(chips.at[e], z_recv.at[e])
        top = both[e]
        for k in range(1, n // 2):
            top = jnp.maximum(top, chips[e, k - 1])
        final[e, core] = top
        remote(final.at[e, core], final.at[e, core], f_send.at[e], f_recv.at[e], partner).start()

    def send(e):
        slot = lax.rem(e, 2)

        @pl.when(e + 1 < experts)
        def _():
            for copy in loads(nx, no, nx_sem, no_sem, e + 1):
                copy.start()

        for copy in loads(nx, no, nx_sem, no_sem, e):
            copy.wait()
        remote(final.at[e, core], final.at[e, core], f_send.at[e], f_recv.at[e], partner).wait()
        for t in range(2):
            for j in range(0, columns, LANES):
                latest = nx[slot, t, :, j : j + LANES] + no[slot, t, :, j : j + LANES].astype(jnp.float32)
                turned[j : j + LANES, :] = (latest / final[e, t, :, j : j + LANES]).T

            @pl.when(e >= 2)
            def _():
                wait_bytes(blocks.at[slot, t, pl.ds(0, n - 1)], send_sem.at[slot, t])
                wait_bytes(blocks.at[slot, t, 0], keep_sem.at[slot, t])

            for d in range(n):
                blocks[slot, t, d] = turned[d * width : (d + 1) * width, :].astype(jnp.bfloat16)
            place = outs[t].at[e, :, pl.ds(pl.multiple_of(me * rows, rows), rows)]
            for k in range(n):
                device = lax.rem(me + n // 2 + k, n)
                block = blocks.at[slot, t, device]
                if k == n // 2:
                    pltpu.make_async_copy(block, place, keep_sem.at[slot, t]).start()
                else:
                    remote(block, place, send_sem.at[slot, t], recv_sem.at[t, e], device).start()

    def step(i, carry):
        pl.when(i < experts)(lambda: measure(i))
        pl.when((i >= 1) & (i < experts + 1))(lambda: chip_max(i - 1))
        pl.when((i >= 2) & (i < experts + 2))(lambda: all_max(i - 2))
        pl.when(i >= DEPTH)(lambda: send(i - DEPTH))
        return carry

    lax.fori_loop(0, experts + DEPTH, step, 0)
    keep = pltpu.make_async_copy(final, scales, s_sem)
    keep.start()
    for slot in range(2):
        for t in range(2):
            wait_bytes(blocks.at[slot, t, pl.ds(0, n - 1)], send_sem.at[slot, t])
            wait_bytes(blocks.at[slot, t, 0], keep_sem.at[slot, t])

    def arrive(e, carry):
        for t in range(2):
            wait_bytes(outs[t].at[e, :, pl.ds(0, (n - 1) * rows)], recv_sem.at[t, e])
        return carry

    lax.fori_loop(0, experts, arrive, 0)
    keep.wait()


def per_device(n, train_gate, other_gate, train_up, other_up, router_weight, router_gain):
    experts, rows, columns = train_gate.shape
    width = columns // n
    f32, bf16, dma = jnp.float32, jnp.bfloat16, pltpu.SemaphoreType.DMA
    ready = jax.ShapeDtypeStruct((experts, width, rows * n), bf16)
    any_space = pl.BlockSpec(memory_space=pl.ANY)
    ready_gate, ready_up, scales = pl.pallas_call(
        functools.partial(regroup, n),
        out_shape=(ready, ready, jax.ShapeDtypeStruct((experts, 2, 1, columns), f32)),
        in_specs=[any_space] * 4,
        out_specs=(any_space,) * 3,
        scratch_shapes=[
            pltpu.VMEM((2, 2, rows, columns), f32),
            pltpu.VMEM((2, 2, rows, columns), bf16),
            pltpu.VMEM((2, 2, rows, columns), f32),
            pltpu.VMEM((2, 2, rows, columns), bf16),
            pltpu.VMEM((columns, rows), f32),
            pltpu.VMEM((2, 2, n, width, rows), bf16),
            pltpu.VMEM((experts, 2, 1, columns), f32),
            pltpu.VMEM((experts, 1, columns), f32),
            pltpu.VMEM((experts, 1, columns), f32),
            pltpu.VMEM((experts, n // 2 - 1, 1, columns), f32),
            pltpu.VMEM((experts, 2, 1, columns), f32),
            dma((2, 2)),
            dma((2, 2)),
            dma((2, 2)),
            dma((2, 2)),
            dma((2, 2)),
            dma((2, 2)),
            dma((2, experts)),
            dma((experts,)),
            dma((experts,)),
            dma((experts,)),
            dma((experts,)),
            dma((experts,)),
            dma((experts,)),
            dma,
        ],
        compiler_params=pltpu.CompilerParams(collective_id=0, has_side_effects=True, vmem_limit_bytes=48 * 2**20),
        name="regroup",
    )(train_gate, other_gate, train_up, other_up)
    ready_gate, ready_up = jnp.swapaxes(ready_gate, 1, 2), jnp.swapaxes(ready_up, 1, 2)
    mine = lax.dynamic_slice_in_dim(scales, lax.axis_index("fsdp") * width, width, axis=3)
    part_router = (router_weight * router_gain[:, None]).astype(jnp.bfloat16)
    row_router = lax.all_gather(part_router, "fsdp", axis=0, tiled=True)
    serve_router = lax.all_gather(row_router, "ep", axis=1, tiled=True)
    return (ready_gate, ready_up, mine[:, 0, 0], mine[:, 1, 0], serve_router)


def solution(mesh):
    in_specs = (
        P("ep", "fsdp", None),
        P("ep", "fsdp", None),
        P("ep", "fsdp", None),
        P("ep", "fsdp", None),
        P("fsdp", "ep"),
        P("fsdp"),
    )
    out_specs = (
        P("ep", None, "fsdp"),
        P("ep", None, "fsdp"),
        P("ep", "fsdp"),
        P("ep", "fsdp"),
        P(),
    )
    return jax.shard_map(
        functools.partial(per_device, mesh.shape["fsdp"]), mesh=mesh, in_specs=in_specs, out_specs=out_specs,
        check_vma=False,
    )
```

time: 812 us -> 558 us (0.69)
  Pallas kernels: 0 us -> 516 us
  blocking collectives: 521 us -> 23.2 us
  local copies, waits for them, and re-layouts: 142 us -> 17.1 us
  waiting for transfers between devices: 64.2 us -> 0 us
  other arithmetic: 63 us -> 0.01 us
  between operations: 14.1 us -> 0.69 us
    pallas_call x0 -> x1, Pallas kernels: none -> 516 us  [per_device(): pl.pallas_call(functools.partial(regroup, n), out_shape=(ready, ready, ja...]
    all_to_all x1 -> x0, blocking collectives: 255 us -> none  [per_device(): lax.all_to_all(narrow_gate, 'fsdp', split_axis=2, concat_axis=1, tiled=True)]
    all_gather x1, blocking collectives: 257 us -> 14 us  [per_device(): row_router = lax.all_gather(part_router, 'fsdp', axis=0, tiled=True)]
    unnamed x15 -> x14, local copies, waits for them, and re-layouts: 82.2 us -> 16.9 us
    pmax x1 -> x0, waiting for transfers between devices: 64.1 us -> none  [per_device(): lax.pmax((jnp.max(jnp.abs(latest_gate), axis=1), jnp.max(jnp.abs(latest_u...]
    all_to_all x4 -> x0, local copies, waits for them, and re-layouts: 58.6 us -> none  [the longest x2 29.3 us: per_device(): lax.all_to_all(narrow_up, 'fsdp', split_axis=2, concat_axis=1, tiled=True)]
    reduce_max x2 -> x0, other arithmetic: 35.7 us -> none  [the longest x1 20.8 us: per_device(): jnp.max(jnp.abs(latest_up), axis=1)]
    convert_element_type x1 -> x0, other arithmetic: 27.3 us -> none  [per_device(): (latest_up / jnp.expand_dims(scale_up, 1)).astype(jnp.bfloat16)]
  transfers between devices with their start and end apart: 2 -> 0, of which waited for: 1 -> 0; matrix products, arithmetic and copies ran while one was open for 2% -> 0% of each run, Pallas kernels for 0% -> 0%
where the time goes in v1:
time: 558 us; the launch traced here: 557 us
  Pallas kernels  516 us (92%)
  blocking collectives  23.2 us (4%)
  local copies, waits for them, and re-layouts  17.1 us (3%)
    pallas_call x1, Pallas kernels, per_device(): pl.pallas_call(functools.partial(regroup, n), out_shape=(ready, ready, ja...  516 us
    unnamed x14, local copies, waits for them, and re-layouts  16.9 us
    all_gather x1, blocking collectives, per_device(): row_router = lax.all_gather(part_router, 'fsdp', axis=0, tiled=True)  14 us

profile of v1, /device:TPU:0, one launch (start us, length us, event | category | flops | bytes accessed | tf_op | source)
XLA Modules:
  0.0 557.5 jit_solution(14995298529279927004)
XLA Ops:
  0.6 0.0 copy-start
  0.6 0.0 copy-start.1
  0.7 516.5 %regroup.1 = (bf16[16,176,2048]{2,1,0:T(8,128)(2,1)}, bf16[16,176,2048]{2,1,0:T(8,128)(2,1)}, f32[16,2,1,1408]{3,2,1,0:T(1,128)S(1)}) custom-call(f32[16,256,1408]{2,1,0:T(8,128)} %tg.1, bf16[16,256,1408]{2,1,0:T(8,128)(2,1)} %og.1, f32[16,256,1408]{2,1,0:T(8,128)} %tu.1, bf16[16,256,1408]{2,1,0:T(8,128)(2,1)} %ou.1), custom_call_target="tpu_custom_call" | custom-call | tf_op jit(solution)/shard_map/regroup/pallas_call | solution.py:143
  517.2 0.1 constant_dynamic-slice_fusion.1
  517.3 0.6 copy_bitcast_fusion
  517.9 0.0 copy-done
  517.9 0.0 copy-done.1
  517.9 14.0 %all_gather.6 = bf16[2048,16]{0,1:T(8,128)(2,1)S(1)} all-gather(bf16[256,16]{0,1:T(8,128)(2,1)S(1)} %multiply_convert_fusion), channel_id=1, replica_groups=mesh['ep'=4,'fsdp'=8] {'fsdp'}, dimensions={0}, use_global_device_ids=true | all-gather | bytes 73728 | tf_op jit(solution)/shard_map/all_gather | solution.py:181
  531.9 0.0 slice-start
  531.9 9.2 %all_gather.7 = bf16[2048,64]{0,1:T(8,128)(2,1)S(1)} all-gather(bf16[2048,16]{0,1:T(8,128)(2,1)S(1)} %all_gather.6), channel_id=1, replica_groups=mesh['ep'=4,'fsdp'=8] {'ep'}, dimensions={1}, use_global_device_ids=true | all-gather | bytes 327680 | tf_op jit(solution)/shard_map/all_gather | solution.py:182
  541.1 0.0 slice-start.1
  541.1 0.0 slice-start.2
  541.1 11.2 %copy.18 = bf16[16,2048,176]{1,2,0:T(8,128)(2,1)} copy(bf16[16,2048,176]{1,2,0:T(8,128)(2,1)} %bitcast.9) | data formatting | bytes 23068672
  552.3 0.0 slice-done
  552.3 0.0 slice-done.1
  552.3 0.0 slice-done.2
  552.3 4.4 copy.19
  556.8 0.7 copy.20
  (2 shorter events, 0.0 us)
Async XLA Ops:
  0.6 517.3 %copy-start = (f32[256,16]{0,1:T(8,128)S(1)}, f32[256,16]{0,1:T(8,128)}, u32[]{:S(2)}) copy-start(f32[256,16]{0,1:T(8,128)} %param.10) | copy-start | bytes 49156
  0.6 517.3 %copy-start.1 = (f32[256]{0:T(256)S(1)}, f32[256]{0:T(256)}, u32[]{:S(2)}) copy-start(f32[256]{0:T(256)} %param.11) | copy-start | bytes 3076
  531.9 20.4 %slice-start = ((s8[11534336]{0:T(1024)(128)(4,1)}), s8[4194304]{0:T(1024)(128)(4,1)S(1)}, s32[]{:S(2)}) async-start(s8[11534336]{0:T(1024)(128)(4,1)} %bitcast.6), calls=%async_computation | async-start | bytes 8388608
  541.1 11.2 %slice-start.1 = ((s8[11534336]{0:T(1024)(128)(4,1)}), s8[4194304]{0:T(1024)(128)(4,1)S(1)}, s32[]{:S(2)}) async-start(s8[11534336]{0:T(1024)(128)(4,1)} %bitcast.6), calls=%async_computation.1 | async-start | bytes 8388608
  541.1 11.2 %slice-start.2 = ((s8[11534336]{0:T(1024)(128)(4,1)}), s8[3145728]{0:T(1024)(128)(4,1)S(1)}, s32[]{:S(2)}) async-start(s8[11534336]{0:T(1024)(128)(4,1)} %bitcast.6), calls=%async_computation.2 | async-start | bytes 6291456

commit v2 on v1

--- a/solution.py
+++ b/solution.py
@@ -11,9 +11,10 @@
 DEPTH = 3
 
 
-def regroup(n, tg, og, tu, ou, rg, ru, scales, mx, mo, nx, no, turned, blocks, own, pair, both, chips, final,
-            mx_sem, mo_sem, nx_sem, no_sem, send_sem, keep_sem, recv_sem, p_send, p_recv, z_send, z_recv, f_send, f_recv, s_sem):
-    me = lax.axis_index("fsdp")
+def regroup(n, teams, tg, og, tu, ou, part, rg, ru, scales, router, mx, mo, nx, no, turned, blocks, own, pair, both, chips, final,
+            mx_sem, mo_sem, nx_sem, no_sem, send_sem, keep_sem, recv_sem, p_send, p_recv, z_send, z_recv, f_send, f_recv, s_sem,
+            row, whole, a_send, a_recv, a_keep, b_send, b_recv, b_keep):
+    me, team = lax.axis_index("fsdp"), lax.axis_index("ep")
     core = lax.rem(me, 2)
     partner = me + 1 - 2 * core
     experts, rows, columns = tg.shape
@@ -45,7 +46,9 @@
     barrier = pltpu.get_barrier_semaphore()
     for k in range(1, n):
         pl.semaphore_signal(barrier, inc=1, device_id={"fsdp": lax.rem(me + k, n)}, device_id_type=pl.DeviceIdType.MESH)
-    pl.semaphore_wait(barrier, n - 1)
+    for k in range(1, teams):
+        pl.semaphore_signal(barrier, inc=1, device_id={"ep": lax.rem(team + k, teams)}, device_id_type=pl.DeviceIdType.MESH)
+    pl.semaphore_wait(barrier, n + teams - 2)
 
     def measure(e):
         slot = lax.rem(e, 2)
@@ -110,16 +113,39 @@
                 else:
                     remote(block, place, send_sem.at[slot, t], recv_sem.at[t, e], device).start()
 
+    def router_rows():
+        pltpu.make_async_copy(part, row.at[me], a_keep).start()
+        for k in range(1, n):
+            remote(part, row.at[me], a_send, a_recv, lax.rem(me + k, n)).start()
+
+    def router_columns():
+        pltpu.make_async_copy(part, row.at[me], a_keep).wait()
+        wait_bytes(row.at[pl.ds(0, n - 1)], a_send)
+        wait_bytes(row.at[pl.ds(0, n - 1)], a_recv)
+        pltpu.make_async_copy(row, whole.at[team], b_keep).start()
+        for k in range(1, teams):
+            pltpu.make_async_remote_copy(
+                src_ref=row, dst_ref=whole.at[team], send_sem=b_send, recv_sem=b_recv,
+                device_id={"ep": lax.rem(team + k, teams)}, device_id_type=pl.DeviceIdType.MESH,
+            ).start()
+
     def step(i, carry):
+        pl.when(i >= DEPTH)(lambda: send(i - DEPTH))
         pl.when(i < experts)(lambda: measure(i))
         pl.when((i >= 1) & (i < experts + 1))(lambda: chip_max(i - 1))
         pl.when((i >= 2) & (i < experts + 2))(lambda: all_max(i - 2))
-        pl.when(i >= DEPTH)(lambda: send(i - DEPTH))
+        pl.when(i == DEPTH)(router_rows)
+        pl.when(i == experts)(router_columns)
         return carry
 
     lax.fori_loop(0, experts + DEPTH, step, 0)
     keep = pltpu.make_async_copy(final, scales, s_sem)
     keep.start()
+    pltpu.make_async_copy(row, whole.at[team], b_keep).wait()
+    wait_bytes(whole.at[pl.ds(0, teams - 1)], b_send)
+    wait_bytes(whole.at[pl.ds(0, teams - 1)], b_recv)
+    keep_router = pltpu.make_async_copy(whole, router, a_keep)
+    keep_router.start()
     for slot in range(2):
         for t in range(2):
             wait_bytes(blocks.at[slot, t, pl.ds(0, n - 1)], send_sem.at[slot, t])
@@ -132,19 +158,22 @@
 
     lax.fori_loop(0, experts, arrive, 0)
     keep.wait()
-
-
-def per_device(n, train_gate, other_gate, train_up, other_up, router_weight, router_gain):
+    keep_router.wait()
+
+
+def per_device(n, teams, train_gate, other_gate, train_up, other_up, router_weight, router_gain):
     experts, rows, columns = train_gate.shape
     width = columns // n
     f32, bf16, dma = jnp.float32, jnp.bfloat16, pltpu.SemaphoreType.DMA
     ready = jax.ShapeDtypeStruct((experts, width, rows * n), bf16)
     any_space = pl.BlockSpec(memory_space=pl.ANY)
-    ready_gate, ready_up, scales = pl.pallas_call(
-        functools.partial(regroup, n),
-        out_shape=(ready, ready, jax.ShapeDtypeStruct((experts, 2, 1, columns), f32)),
-        in_specs=[any_space] * 4,
-        out_specs=(any_space,) * 3,
+    part_router = (router_weight * router_gain[:, None]).astype(bf16).T
+    ready_gate, ready_up, scales, router = pl.pallas_call(
+        functools.partial(regroup, n, teams),
+        out_shape=(ready, ready, jax.ShapeDtypeStruct((experts, 2, 1, columns), f32),
+                   jax.ShapeDtypeStruct((teams, n) + part_router.shape, bf16)),
+        in_specs=[any_space] * 4 + [pl.BlockSpec(memory_space=pltpu.VMEM)],
+        out_specs=(any_space,) * 4,
         scratch_shapes=[
             pltpu.VMEM((2, 2, rows, columns), f32),
             pltpu.VMEM((2, 2, rows, columns), bf16),
@@ -171,15 +200,21 @@
             dma((experts,)),
             dma((experts,)),
             dma,
+            pltpu.VMEM((n,) + part_router.shape, bf16),
+            pltpu.VMEM((teams, n) + part_router.shape, bf16),
+            dma,
+            dma,
+            dma,
+            dma,
+            dma,
+            dma,
         ],
         compiler_params=pltpu.CompilerParams(collective_id=0, has_side_effects=True, vmem_limit_bytes=48 * 2**20),
         name="regroup",
-    )(train_gate, other_gate, train_up, other_up)
+    )(train_gate, other_gate, train_up, other_up, part_router)
     ready_gate, ready_up = jnp.swapaxes(ready_gate, 1, 2), jnp.swapaxes(ready_up, 1, 2)
     mine = lax.dynamic_slice_in_dim(scales, lax.axis_index("fsdp") * width, width, axis=3)
-    part_router = (router_weight * router_gain[:, None]).astype(jnp.bfloat16)
-    row_router = lax.all_gather(part_router, "fsdp", axis=0, tiled=True)
-    serve_router = lax.all_gather(row_router, "ep", axis=1, tiled=True)
+    serve_router = router.transpose(1, 3, 0, 2).reshape(n * router.shape[3], -1)
     return (ready_gate, ready_up, mine[:, 0, 0], mine[:, 1, 0], serve_router)
 
 
@@ -200,6 +235,6 @@
         P(),
     )
     return jax.shard_map(
-        functools.partial(per_device, mesh.shape["fsdp"]), mesh=mesh, in_specs=in_specs, out_specs=out_specs,
+        functools.partial(per_device, mesh.shape["fsdp"], mesh.shape["ep"]), mesh=mesh, in_specs=in_specs, out_specs=out_specs,
         check_vma=False,
     )

time: 558 us -> 538 us (0.964)
  blocking collectives: 23.2 us -> 0 us
    all_gather x2 -> x0, blocking collectives: 23.2 us -> none  [the longest x1 14 us: per_device(): row_router = lax.all_gather(part_router, 'fsdp', axis=0, tiled=True)]
    unnamed x14 -> x10, local copies, waits for them, and re-layouts: 16.9 us -> 17.4 us
where the time goes in v2:
time: 538 us
  Pallas kernels  519 us (96%)
  local copies, waits for them, and re-layouts  17.7 us (3%)
    pallas_call x1, Pallas kernels, per_device(): pl.pallas_call(functools.partial(regroup, n, teams), out_shape=(ready, re...  519 us
    unnamed x10, local copies, waits for them, and re-layouts  17.4 us

profile of v2, /device:TPU:0, one launch (start us, length us, event | category | flops | bytes accessed | tf_op | source)
XLA Modules:
  0.0 537.9 jit_solution(8379357152673201010)
XLA Ops:
  0.6 0.7 fusion.part
  1.4 518.8 %regroup.1 = (bf16[16,176,2048]{2,1,0:T(8,128)(2,1)}, bf16[16,176,2048]{2,1,0:T(8,128)(2,1)}, f32[16,2,1,1408]{3,2,1,0:T(1,128)S(1)}, bf16[4,8,16,256]{3,2,1,0:T(8,128)(2,1)S(1)}) custom-call(f32[16,256,1408]{2,1,0:T(8,128)} %tg.1, bf16[16,256,1408]{2,1,0:T(8,128)(2,1)} %og.1, f32[16,256,1408]{2,1,0:T(8,128)} %tu.1, bf16[16,256,1408]{2,1,0:T(8,128)(2,1)} %ou.1, ...), custom_call_target="tpu_custom_call" | custom-call | tf_op jit(solution)/shard_map/regroup/pallas_call | solution.py:171
  520.2 0.1 constant_dynamic-slice_fusion.1
  520.3 0.6 copy_bitcast_fusion
  520.9 0.1 copy.11
  521.0 0.0 slice-start
  521.0 0.8 copy.14
  521.8 0.0 slice-start.1
  521.8 0.0 slice-start.2
  521.8 11.6 %copy.19 = bf16[16,2048,176]{1,2,0:T(8,128)(2,1)} copy(bf16[16,2048,176]{1,2,0:T(8,128)(2,1)} %bitcast.18) | data formatting | bytes 23068672
  533.4 0.0 slice-done
  533.4 0.0 slice-done.1
  533.4 0.0 slice-done.2
  533.4 4.4 copy.20
  (1 shorter events, 0.0 us)
Async XLA Ops:
  521.0 12.4 %slice-start = ((s8[11534336]{0:T(1024)(128)(4,1)}), s8[4194304]{0:T(1024)(128)(4,1)S(1)}, s32[]{:S(2)}) async-start(s8[11534336]{0:T(1024)(128)(4,1)} %bitcast.15), calls=%async_computation | async-start | bytes 8388608
  521.8 11.6 %slice-start.1 = ((s8[11534336]{0:T(1024)(128)(4,1)}), s8[4194304]{0:T(1024)(128)(4,1)S(1)}, s32[]{:S(2)}) async-start(s8[11534336]{0:T(1024)(128)(4,1)} %bitcast.15), calls=%async_computation.1 | async-start | bytes 8388608
  521.8 11.6 %slice-start.2 = ((s8[11534336]{0:T(1024)(128)(4,1)}), s8[3145728]{0:T(1024)(128)(4,1)S(1)}, s32[]{:S(2)}) async-start(s8[11534336]{0:T(1024)(128)(4,1)} %bitcast.15), calls=%async_computation.2 | async-start | bytes 6291456
